TPU v7x, 512 devices: a whole 4x4x16 slice. The times are simulated.
512 devices in a mesh: role: 4 (over z_lo), tp: 4 (over x), dp: 32 (over y, z_hi, core).
Axes of the slice: x: 4, y: 4, z: 16 (z_hi: 4, z_lo: 4; z = z_hi * 4 + z_lo), core: 2. Of those that a mesh axis runs over, the one named last changes fastest.
Arguments:
- master: float32 [1024, 8192], P('tp', ('role', 'dp')), may hold values from -0.0625 to 0.0625
- key_bias: float32 [1024], P('tp'), may hold values from -3 to 3
- probe_tokens: bfloat16 [32768, 8192], P(('role', 'dp')), may hold values from -6 to 6
Outputs:
- weight: bfloat16 [8192, 1024], P(None, 'tp')
- probe_keys: bfloat16 [32768, 1024], P(('role', 'dp'), 'tp')
- checksum: float32 [8192], replicated
All inputs are finite; a program needn't handle non-finite values.
Results may differ from a plain program's by a relative error of at most 0.005.
Values may be sent and summed in bfloat16 or wider, within the bound.
No kernel may reach another device: no remote copies, remote signals or barrier semaphores. Data moves between devices by JAX's collectives and lax.ppermute only.
A program may use at most 64 MiB of HBM per device.

v0:
```python
import jax
import jax.numpy as jnp
from jax import lax
from jax.sharding import PartitionSpec as P


def copy_for_each(value, axis):
    copies = jnp.broadcast_to(value, (lax.axis_size(axis), *value.shape))
    return lax.all_to_all(copies, axis, split_axis=0, concat_axis=0, tiled=True)


def over_copies(value, axis):
    return copy_for_each(value, axis).sum(axis=0)


def body(master, key_bias, probe_tokens):
    own_rows = jnp.transpose(master).astype(jnp.bfloat16)
    replica_block = lax.all_gather(own_rows, "dp", axis=0, tiled=True)
    incoming = lax.all_gather(replica_block, "role", axis=0, tiled=True)
    totals = jnp.dot(probe_tokens, incoming, preferred_element_type=jnp.float32)
    probe_keys = (totals + key_bias[None, :]).astype(jnp.bfloat16)
    checksum = over_copies(jnp.sum(incoming.astype(jnp.float32), axis=1), "tp")
    return (incoming, probe_keys, checksum)


def solution(mesh):
    placed = (P("tp", ("role", "dp")), P("tp"), P(("role", "dp"), None))
    return jax.shard_map(
        body,
        mesh=mesh,
        in_specs=placed,
        out_specs=(P(None, "tp"), P(("role", "dp"), "tp"), P()),
        check_vma=False,
    )
```

profile of v0, /device:TPU:2, one launch (start us, length us, event | category | flops | bytes accessed | tf_op | source)
XLA Modules:
  0.0 199.0 jit_solution(13851942847966646415)
XLA Ops:
  7.2 0.0 copy-start
  7.2 0.0 all-gather.3.cloned.1.call-start
  7.2 1.5 convert_bitcast_fusion
  8.7 0.0 all-gather.3.cloned.1.call-update
  8.7 0.0 all-gather.5.cloned.1.call-start
  8.8 79.2 %all-gather.3.cloned.1.call-done = bf16[2048,256]{1,0:T(8,128)(2,1)} async-done(((bf16[64,256]{1,0:T(8,128)(2,1)}), bf16[2048,256]{1,0:T(8,128)(2,1)}) %all-gather.3.cloned.1.call-update) | async-done | bytes 1048592 | tf_op jit(solution)/shard_map/all_gather | solution.py:18
  87.9 0.0 all-gather.5.cloned.1.call-update
  88.0 84.8 %all-gather.5.cloned.1.call-done = bf16[8192,256]{1,0:T(8,128)(2,1)} async-done(((bf16[2048,256]{1,0:T(8,128)(2,1)}), bf16[8192,256]{1,0:T(8,128)(2,1)}) %all-gather.5.cloned.1.call-update) | async-done | bytes 4194320 | tf_op jit(solution)/shard_map/all_gather | solution.py:19
  172.7 3.3 %convert_reduce_fusion = f32[8192]{0:T(1024)S(1)} fusion(bf16[8192,256]{1,0:T(8,128)(2,1)} %all-gather.5.cloned.1.call-done), kind=kLoop, calls=%fused_computation | loop fusion | flops 4186112 | bytes 4227072 | tf_op jit(solution)/shard_map/reduce_sum | solution.py:22
  176.1 0.7 broadcast_in_dim.4
  176.8 4.8 %all-to-all-start = ((f32[4,1,8192]{2,1,0:T(1,128)}), f32[4,1,8192]{2,1,0:T(1,128)S(1)}, u32[]{:S(2)}, u32[]{:S(2)}) async-start(f32[4,1,8192]{2,1,0:T(1,128)} %broadcast_in_dim.4), calls=%async_computation | async-start | bytes 262144 | tf_op jit(solution)/shard_map/all_to_all | solution.py:9
  181.6 0.0 copy-done
  181.6 5.4 %fusion = bf16[256,256]{1,0:T(8,128)(2,1)} fusion(bf16[256,8192]{1,0:T(8,128)(2,1)} %param.5, bf16[8192,256]{1,0:T(8,128)(2,1)} %all-gather.5.cloned.1.call-done, f32[256]{0:T(256)S(1)} %copy-done), kind=kOutput, calls=%fused_computation.2 | convolution fusion | flops 1073872896 | bytes 8520704 | tf_op jit(solution)/shard_map/dot_general | solution.py:20
  187.0 0.0 all-to-all-done
  187.0 0.7 reduce_sum.19
  187.7 4.5 %copy.9 = bf16[8192,256]{1,0:T(8,128)(2,1)} copy(bf16[8192,256]{1,0:T(8,128)(2,1)} %all-gather.5.cloned.1.call-done) | data formatting | bytes 8388608
Async XLA Ops:
  7.2 174.4 %copy-start = (f32[256]{0:T(256)S(1)}, f32[256]{0:T(256)}, u32[]{:S(2)}) copy-start(f32[256]{0:T(256)} %param.4) | copy-start | bytes 3076
  7.2 80.8 %all-gather.3.cloned.1.call-start = ((), (), s32[]{:S(2)}) async-start(), calls=%async_computation.1 | async-start | bytes 1081344 | tf_op jit(solution)/shard_map/all_gather | solution.py:18
  8.7 164.0 %all-gather.5.cloned.1.call-start = ((), (), s32[]{:S(2)}) async-start(), calls=%async_computation.2 | async-start | bytes 5242880 | tf_op jit(solution)/shard_map/all_gather | solution.py:19
  176.8 10.2 %all-to-all-start = ((f32[4,1,8192]{2,1,0:T(1,128)}), f32[4,1,8192]{2,1,0:T(1,128)S(1)}, u32[]{:S(2)}, u32[]{:S(2)}) async-start(f32[4,1,8192]{2,1,0:T(1,128)} %broadcast_in_dim.4), calls=%async_computation | async-start | bytes 262144 | tf_op jit(solution)/shard_map/all_to_all | solution.py:9
Sparse Core Ops, SparseCore 0:
  11.7 76.1 all-gather.2
  90.0 82.6 all-gather.4
where the time goes:
time: 199 us
  waiting for transfers between devices  164 us (82%)
  between operations  14.1 us (7%)
  other arithmetic  5.54 us (3%)
  matrix products  5.37 us (3%)
  local copies, waits for them, and re-layouts  5.2 us (3%)
  starting transfers between devices  4.88 us (2%)
    all_gather x1, waiting for transfers between devices, body(): incoming = lax.all_gather(replica_block, 'role', axis=0, tiled=True)  84.8 us
    all_gather x1, waiting for transfers between devices, body(): replica_block = lax.all_gather(own_rows, 'dp', axis=0, tiled=True)  79.2 us
    dot_general x1, matrix products, body(): totals = jnp.dot(probe_tokens, incoming, preferred_element_type=jnp.float32)  5.37 us
    all_to_all x1, starting transfers between devices, copy_for_each(): return lax.all_to_all(copies, axis, split_axis=0, concat_axis=0, tiled=True)  4.8 us
    unnamed x3, local copies, waits for them, and re-layouts  4.47 us
  transfers between devices with their start and end apart: 3, of which 2 were waited for; matrix products, arithmetic and copies ran while one was open for 3% of the time, Pallas kernels for 0%

commit v1 on v0

--- a/solution.py
+++ b/solution.py
@@ -2,6 +2,11 @@
 import jax.numpy as jnp
 from jax import lax
 from jax.sharding import PartitionSpec as P
+
+
+def swapped_in(shard, axis, dim):
+    sent = jnp.stack([shard] * lax.axis_size(axis))
+    return jnp.concatenate(lax.all_to_all(sent, axis, 0, 0), axis=dim)
 
 
 def copy_for_each(value, axis):
@@ -16,7 +21,7 @@
 def body(master, key_bias, probe_tokens):
     own_rows = jnp.transpose(master).astype(jnp.bfloat16)
     replica_block = lax.all_gather(own_rows, "dp", axis=0, tiled=True)
-    incoming = lax.all_gather(replica_block, "role", axis=0, tiled=True)
+    incoming = swapped_in(replica_block, "role", 0)
     totals = jnp.dot(probe_tokens, incoming, preferred_element_type=jnp.float32)
     probe_keys = (totals + key_bias[None, :]).astype(jnp.bfloat16)
     checksum = over_copies(jnp.sum(incoming.astype(jnp.float32), axis=1), "tp")

time: 199 us -> 212 us (1.065)
  blocking collectives: 0 us -> 96.4 us
  waiting for transfers between devices: 164 us -> 79.2 us
  local copies, waits for them, and re-layouts: 5.2 us -> 8.63 us
  other arithmetic: 5.54 us -> 3.37 us
    all_to_all x0 -> x1, blocking collectives: none -> 96.4 us  [swapped_in(): return jnp.concatenate(lax.all_to_all(sent, axis, 0, 0), axis=dim)]
    all_gather x1 -> x0, waiting for transfers between devices: 84.8 us -> none  [body(): incoming = lax.all_gather(replica_block, 'role', axis=0, tiled=True)]
    reduce_sum x1, other arithmetic: 3.34 us -> 1.17 us  [body(): checksum = over_copies(jnp.sum(incoming.astype(jnp.float32), axis=1), 'tp')]
    unnamed x3 -> x6, local copies, waits for them, and re-layouts: 4.47 us -> 6.41 us
  transfers between devices with their start and end apart: 3 -> 2, of which waited for: 2 -> 1; matrix products, arithmetic and copies ran while one was open for 3% -> 3% of each run, Pallas kernels for 0% -> 0%
where the time goes in v1:
time: 212 us
  blocking collectives  96.4 us (45%)
  waiting for transfers between devices  79.2 us (37%)
  between operations  14 us (7%)
  local copies, waits for them, and re-layouts  8.63 us (4%)
  matrix products  5.37 us (3%)
  starting transfers between devices  4.84 us (2%)
  other arithmetic  3.37 us (2%)
    all_to_all x1, blocking collectives, swapped_in(): return jnp.concatenate(lax.all_to_all(sent, axis, 0, 0), axis=dim)  96.4 us
    all_gather x1, waiting for transfers between devices, body(): replica_block = lax.all_gather(own_rows, 'dp', axis=0, tiled=True)  79.2 us
    unnamed x6, local copies, waits for them, and re-layouts  6.41 us
    dot_general x1, matrix products, body(): totals = jnp.dot(probe_tokens, incoming, preferred_element_type=jnp.float32)  5.37 us
    all_to_all x1, starting transfers between devices, copy_for_each(): return lax.all_to_all(copies, axis, split_axis=0, concat_axis=0, tiled=True)  4.8 us
  transfers between devices with their start and end apart: 2, of which 1 were waited for; matrix products, arithmetic and copies ran while one was open for 3% of the time, Pallas kernels for 0%

profile of v1, /device:TPU:2, one launch (start us, length us, event | category | flops | bytes accessed | tf_op | source)
XLA Modules:
  0.0 211.9 jit_solution(2521690471913628261)
XLA Ops:
  7.2 0.0 all-gather.2.cloned.1.call-start
  7.2 1.5 convert_bitcast_fusion
  8.7 0.0 all-gather.2.cloned.1.call-update
  8.7 79.2 %all-gather.2.cloned.1.call-done = bf16[2048,256]{1,0:T(8,128)(2,1)} async-done(((bf16[64,256]{1,0:T(8,128)(2,1)}), bf16[2048,256]{1,0:T(8,128)(2,1)}) %all-gather.2.cloned.1.call-update) | async-done | bytes 1048592 | tf_op jit(solution)/shard_map/all_gather | solution.py:23
  87.9 1.5 stack.2
  89.4 96.4 %all_to_all.11 = bf16[4,2048,256]{2,1,0:T(8,128)(2,1)S(1)} all-to-all(bf16[4,2048,256]{2,1,0:T(8,128)(2,1)S(1)} %stack.2), channel_id=1, replica_groups=mesh['role'=4,'tp'=4,'dp'=32] {'role'}, dimensions={0} | all-to-all | bytes 8388608 | tf_op jit(solution)/shard_map/all_to_all | solution.py:9
  185.8 0.0 copy-start
  185.8 1.9 copy-done
  187.7 0.0 copy-start.1
  187.7 1.2 convert_reduce_fusion
  188.9 0.7 broadcast_in_dim.7
  189.6 4.8 %all-to-all-start.1 = ((f32[4,1,8192]{2,1,0:T(1,128)}), f32[4,1,8192]{2,1,0:T(1,128)S(1)}, u32[]{:S(2)}, u32[]{:S(2)}) async-start(f32[4,1,8192]{2,1,0:T(1,128)} %broadcast_in_dim.7), calls=%async_computation.1 | async-start | bytes 262144 | tf_op jit(solution)/shard_map/all_to_all | solution.py:14
  194.4 0.0 copy-done.1
  194.4 5.4 %fusion = bf16[256,256]{1,0:T(8,128)(2,1)} fusion(bf16[256,8192]{1,0:T(8,128)(2,1)} %param.5, bf16[8192,256]{1,0:T(8,128)(2,1)} %bitcast.7, f32[256]{0:T(256)S(1)} %copy-done.1), kind=kOutput, calls=%fused_computation.2 | convolution fusion | flops 1073872896 | bytes 8520704 | tf_op jit(solution)/shard_map/dot_general | solution.py:25
  199.8 0.0 all-to-all-done.1
  199.8 0.7 reduce_sum.19
  200.6 4.5 %copy.10 = bf16[8192,256]{1,0:T(8,128)(2,1)} copy(bf16[8192,256]{1,0:T(8,128)(2,1)} %bitcast.8) | data formatting | bytes 8388608
  (1 shorter events, 0.0 us)
Async XLA Ops:
  7.2 80.8 %all-gather.2.cloned.1.call-start = ((), (), s32[]{:S(2)}) async-start(), calls=%async_computation.2 | async-start | bytes 1081344 | tf_op jit(solution)/shard_map/all_gather | solution.py:23
  185.8 1.9 copy-start
  187.7 6.7 %copy-start.1 = (f32[256]{0:T(256)S(1)}, f32[256]{0:T(256)}, u32[]{:S(2)}) copy-start(f32[256]{0:T(256)} %param.4) | copy-start | bytes 3076
  189.6 10.2 %all-to-all-start.1 = ((f32[4,1,8192]{2,1,0:T(1,128)}), f32[4,1,8192]{2,1,0:T(1,128)S(1)}, u32[]{:S(2)}, u32[]{:S(2)}) async-start(f32[4,1,8192]{2,1,0:T(1,128)} %broadcast_in_dim.7), calls=%async_computation.1 | async-start | bytes 262144 | tf_op jit(solution)/shard_map/all_to_all | solution.py:14
Sparse Core Ops, SparseCore 0:
  11.7 76.1 all-gather.1
